TPU v7x, 128 devices: a whole 4x4x4 slice. The times are simulated.
128 devices in a mesh: depth: 2 (over core), row: 16 (over z, x), col: 4 (over y).
Axes of the slice: x: 4, y: 4, z: 4, core: 2. Of those that a mesh axis runs over, the one named last changes fastest.
Arguments:
- right_side: bfloat16 [4, 16, 8, 128, 512], P(None, 'row', ('depth', 'col')), may hold values from -6 to 6
- inverse_diag: bfloat16 [4, 16, 8, 1, 128, 128], P(None, 'row', ('depth', 'col')), may hold values from -2 to 2.5, as said below
- coupling: bfloat16 [3, 16, 1024, 8, 2048], P(None, 'row', None, ('depth', 'col')), may hold values from -0.0625 to 0.0625
- pattern: int32 [3, 16, 8, 8, 16], P(None, 'row', None, ('depth', 'col')), may hold values 0 or 1
Outputs:
- forward_solution: bfloat16 [4, 16, 8, 128, 512], P(None, 'row', ('depth', 'col'))
- solution: bfloat16 [4, 16, 8, 128, 512], P(None, 'row', ('depth', 'col'))
Inputs may be any that keep to these rules, and one draw needn't show every extreme that they name: `inverse_diag`: each block is lower triangular with positive diagonal.
All inputs are finite; a program needn't handle non-finite values. No bound on the sum of `pattern` on one device may be relied on, other than what follows from the above.
Results may differ from a plain program's by a relative error of at most 0.025.
Values may be sent and summed in bfloat16 or wider, within the bound.
A program may use at most 128 MiB of HBM per device.

v0:
```python
import jax
import jax.numpy as jnp
from jax import lax
from jax.sharding import PartitionSpec as P


def apply_inverse(inverse, vector, transposed):
    blocks_in = vector.reshape(inverse.shape[0], inverse.shape[1], vector.shape[-1])
    einsum_form = "tji,tjn->tin" if transposed else "tij,tjn->tin"
    result = jnp.einsum(einsum_form, inverse, blocks_in, preferred_element_type=jnp.float32)
    return result.astype(jnp.bfloat16).reshape(vector.shape)


def lift_upward(masked, share_in):
    portion = lax.all_gather(share_in, "row", axis=0, tiled=True)
    span_rows = portion.shape[0] * portion.shape[2]
    return jnp.dot(
        masked, portion.reshape(span_rows, portion.shape[-1]), preferred_element_type=jnp.float32
    )


def carry_downward(masked, share_in):
    portion = lax.all_gather(share_in, ("depth", "col"), axis=1, tiled=True)
    span_rows = portion.shape[1] * portion.shape[2]
    return lax.dot_general(
        masked,
        portion.reshape(span_rows, portion.shape[-1]),
        (((0,), (0,)), ((), ())),
        preferred_element_type=jnp.float32,
    )


def forward_sum(partial_value, share_rows):
    blocks = partial_value.reshape(
        lax.axis_size(("depth", "col")), share_rows, partial_value.shape[-1]
    )
    summed = lax.psum(blocks.astype(jnp.bfloat16), ("depth", "col")).astype(jnp.float32)
    return lax.dynamic_index_in_dim(summed, lax.axis_index(("depth", "col")), 0, keepdims=False)


def backward_sum(partial_value, share_rows):
    blocks = partial_value.reshape(lax.axis_size("row"), share_rows, partial_value.shape[-1])
    summed = lax.psum(blocks.astype(jnp.bfloat16), "row").astype(jnp.float32)
    return lax.dynamic_index_in_dim(summed, lax.axis_index("row"), 0, keepdims=False)


def body(right_side, inverse_diag, coupling, pattern):
    levels = right_side.shape[0]
    share_rows = right_side.shape[3]
    rhs_cols = right_side.shape[4]
    block_width = inverse_diag.shape[-1]
    masked = []
    for pair_at in range(levels - 1):
        slab = coupling[pair_at, 0, :, 0, :]
        gate = pattern[pair_at, 0, :, 0, :].astype(jnp.bfloat16)
        shaped = (
            slab.reshape(gate.shape[0], block_width, gate.shape[1], block_width)
            * gate[:, None, :, None]
        )
        masked.append(shaped.reshape(slab.shape))
    panel_spans = [(0, rhs_cols)]
    fwd_levels = []
    for level_at in range(levels):
        pieces = []
        for panel_at, (col_first, col_last) in enumerate(panel_spans):
            source = right_side[level_at, 0, 0, :, col_first:col_last]
            if level_at == 0:
                residual = source
            else:
                partial_value = lift_upward(
                    masked[level_at - 1], fwd_levels[level_at - 1][panel_at][None, None]
                )
                residual = (
                    source.astype(jnp.float32) - forward_sum(partial_value, share_rows)
                ).astype(jnp.bfloat16)
            pieces.append(apply_inverse(inverse_diag[level_at, 0, 0], residual, False))
        fwd_levels.append(pieces)
    bwd_levels = [None] * levels
    for level_at in reversed(range(levels)):
        pieces = []
        panel_at = 0
        known_part = fwd_levels[level_at][panel_at]
        if level_at == levels - 1:
            residual = known_part
        else:
            partial_value = carry_downward(
                masked[level_at], bwd_levels[level_at + 1][panel_at][None, None]
            )
            residual = (
                known_part.astype(jnp.float32) - backward_sum(partial_value, share_rows)
            ).astype(jnp.bfloat16)
        pieces.append(apply_inverse(inverse_diag[level_at, 0, 0], residual, True))
        bwd_levels[level_at] = pieces
    forward_rows = []
    backward_rows = []
    for level_at in range(levels):
        forward_rows.append(jnp.concatenate(fwd_levels[level_at], axis=1))
        backward_rows.append(jnp.concatenate(bwd_levels[level_at], axis=1))
    forward_solution = jnp.stack(forward_rows).reshape(levels, 1, 1, share_rows, rhs_cols)
    solution = jnp.stack(backward_rows).reshape(levels, 1, 1, share_rows, rhs_cols)
    return (forward_solution, solution)


def solution(mesh):
    placed = (
        P(None, "row", ("depth", "col"), None, None),
        P(None, "row", ("depth", "col"), None, None, None),
        P(None, "row", None, ("depth", "col"), None),
        P(None, "row", None, ("depth", "col"), None),
    )
    return jax.shard_map(
        body,
        mesh=mesh,
        in_specs=placed,
        out_specs=(
            P(None, "row", ("depth", "col"), None, None),
            P(None, "row", ("depth", "col"), None, None),
        ),
        check_vma=False,
    )
```

profile of v0, /device:TPU:0, one launch (start us, length us, event | category | flops | bytes accessed | tf_op | source)
XLA Modules:
  0.0 735.9 jit_solution(18099699853977080136)
XLA Ops:
  12.3 7.3 mul.63
  22.2 7.3 mul.72
  32.2 7.4 mul.68
  39.5 13.6 %slice_multiply_fusion.2 = (bf16[1,1,1024,1,2048]{4,2,3,1,0:T(8,128)(2,1)}, bf16[1,1,1024,1,2048]{4,2,3,1,0:T(8,128)(2,1)}, bf16[1,1,1024,1,2048]{4,2,3,1,0:T(8,128)(2,1)}) fusion(bf16[1,1,1024,1,2048]{4,2,3,1,0:T(8,128)(2,1)} %mul.63, bf16[3,1,1024,1,2048]{4,2,3,1,0:T(8,128)(2,1)} %param.6, bf16[1,1,1024,1,2048]{4,2,3,1,0:T(8,128)(2,1)} %mul.72, ...), kind=kLoop, calls=%fused_computation.8 | loop fusion | flops 6291456 | bytes 37748736 | tf_op jit(solution)/shard_map/mul | solution.py:57
  58.2 6.2 fusion.9
  64.5 62.1 %all-reduce.7.cloned.1.call-done = bf16[8,128,512]{2,1,0:T(8,128)(2,1)} async-done(((bf16[8,128,512]{2,1,0:T(8,128)(2,1)}), bf16[8,128,512]{2,1,0:T(8,128)(2,1)}) %all-reduce.7.cloned.1.call-update) | async-done | bytes 1048592 | tf_op jit(solution)/shard_map/psum | solution.py:37
  128.5 45.3 %all-gather.15.cloned.1.call-done = bf16[2048,512]{1,0:T(8,128)(2,1)} async-done(((bf16[128,512]{1,0:T(8,128)(2,1)}), bf16[2048,512]{1,0:T(8,128)(2,1)}) %all-gather.15.cloned.1.call-update) | async-done | bytes 2097168 | tf_op jit(solution)/shard_map/all_gather | solution.py:15
  173.7 6.2 fusion.12
  180.0 62.1 %all-reduce.9.cloned.1.call-done = bf16[8,128,512]{2,1,0:T(8,128)(2,1)} async-done(((bf16[8,128,512]{2,1,0:T(8,128)(2,1)}), bf16[8,128,512]{2,1,0:T(8,128)(2,1)}) %all-reduce.9.cloned.1.call-update) | async-done | bytes 1048592 | tf_op jit(solution)/shard_map/psum | solution.py:37
  243.9 44.5 %all-gather.17.cloned.1.call-done = bf16[2048,512]{1,0:T(8,128)(2,1)} async-done(((bf16[128,512]{1,0:T(8,128)(2,1)}), bf16[2048,512]{1,0:T(8,128)(2,1)}) %all-gather.17.cloned.1.call-update) | async-done | bytes 2097168 | tf_op jit(solution)/shard_map/all_gather | solution.py:15
  288.5 6.2 fusion.15
  294.7 62.1 %all-reduce.11.cloned.1.call-done = bf16[8,128,512]{2,1,0:T(8,128)(2,1)} async-done(((bf16[8,128,512]{2,1,0:T(8,128)(2,1)}), bf16[8,128,512]{2,1,0:T(8,128)(2,1)}) %all-reduce.11.cloned.1.call-update) | async-done | bytes 1048592 | tf_op jit(solution)/shard_map/psum | solution.py:37
  359.0 15.1 %fusion.2 = (bf16[2048,1024]{0,1:T(8,128)(2,1)}, bf16[2048,1024]{0,1:T(8,128)(2,1)}, bf16[2048,1024]{0,1:T(8,128)(2,1)}) fusion(bf16[128,8,16,128]{3,2,1,0:T(8,128)(2,1)} %bitcast.180, bf16[3,1,1024,1,2048]{4,2,3,1,0:T(8,128)(2,1)} %param.6, bf16[128,8,16,128]{3,2,1,0:T(8,128)(2,1)} %bitcast.182, bf16[128,8,16,128]{3,2,1,0:T(8,128)(2,1)} %bitcast.181), kind=kLoop, calls=%fused_computation.5 | loop fusion | flops 6291456 | bytes 37748736 | tf_op jit(solution)/shard_map/dot_general | solution.py:25
  374.1 6.4 copy.26
  381.6 6.3 convolution_convert_fusion.2
  387.9 92.3 %all-reduce.13.cloned.1.call-done = bf16[16,128,512]{2,1,0:T(8,128)(2,1)} async-done(((bf16[16,128,512]{2,1,0:T(8,128)(2,1)}), bf16[16,128,512]{2,1,0:T(8,128)(2,1)}) %all-reduce.13.cloned.1.call-update) | async-done | bytes 2097168 | tf_op jit(solution)/shard_map/psum | solution.py:43
  482.1 6.4 copy.25
  488.5 16.4 %all-gather.21.cloned.1.call-done = bf16[1024,512]{0,1:T(8,128)(2,1)} async-done(((bf16[128,512]{0,1:T(8,128)(2,1)}), bf16[1024,512]{0,1:T(8,128)(2,1)}) %all-gather.21.cloned.1.call-update) | async-done | bytes 1048592 | tf_op jit(solution)/shard_map/all_gather | solution.py:23
  504.9 6.3 convolution_convert_fusion.1
  511.2 92.3 %all-reduce.15.cloned.1.call-done = bf16[16,128,512]{2,1,0:T(8,128)(2,1)} async-done(((bf16[16,128,512]{2,1,0:T(8,128)(2,1)}), bf16[16,128,512]{2,1,0:T(8,128)(2,1)}) %all-reduce.15.cloned.1.call-update) | async-done | bytes 2097168 | tf_op jit(solution)/shard_map/psum | solution.py:43
  605.3 6.4 copy.24
  611.7 16.4 %all-gather.23.cloned.1.call-done = bf16[1024,512]{0,1:T(8,128)(2,1)} async-done(((bf16[128,512]{0,1:T(8,128)(2,1)}), bf16[1024,512]{0,1:T(8,128)(2,1)}) %all-gather.23.cloned.1.call-update) | async-done | bytes 1048592 | tf_op jit(solution)/shard_map/all_gather | solution.py:23
  628.2 6.3 convolution_convert_fusion
  635.3 91.5 %all-reduce.17.cloned.1.call-done = bf16[16,128,512]{2,1,0:T(8,128)(2,1)} async-done(((bf16[16,128,512]{2,1,0:T(8,128)(2,1)}), bf16[16,128,512]{2,1,0:T(8,128)(2,1)}) %all-reduce.17.cloned.1.call-update) | async-done | bytes 2097168 | tf_op jit(solution)/shard_map/psum | solution.py:43
  (58 shorter events, 29.4 us)
Async XLA Ops:
  7.2 51.1 %all-gather.13.cloned.1.call-start = ((), (), s32[]{:S(2)}) async-start(), calls=%async_computation.6 | async-start | bytes 2228224 | tf_op jit(solution)/shard_map/all_gather | solution.py:15
  9.0 117.6 %all-reduce.7.cloned.1.call-start = ((), (), s32[]{:S(2)}) async-start(), calls=%async_computation | async-start | bytes 2097152 | tf_op jit(solution)/shard_map/psum | solution.py:37
  58.2 68.4 %copy-start.6 = (bf16[4,1,1,128,512]{4,3,2,1,0:T(8,128)(2,1)S(1)}, bf16[4,1,1,128,512]{4,3,2,1,0:T(8,128)(2,1)}, u32[]{:S(2)}) copy-start(bf16[4,1,1,128,512]{4,3,2,1,0:T(8,128)(2,1)} %param.4) | copy-start | bytes 1572868
  58.2 68.4 %copy-start.7 = (bf16[4,1,1,1,128,128]{5,4,3,2,1,0:T(8,128)(2,1)S(1)}, bf16[4,1,1,1,128,128]{5,4,3,2,1,0:T(8,128)(2,1)}, u32[]{:S(2)}) copy-start(bf16[4,1,1,1,128,128]{5,4,3,2,1,0:T(8,128)(2,1)} %param.5) | copy-start | bytes 393220
  64.5 109.2 %all-gather.15.cloned.1.call-start = ((), (), s32[]{:S(2)}) async-start(), calls=%async_computation.7 | async-start | bytes 2228224 | tf_op jit(solution)/shard_map/all_gather | solution.py:15
  128.4 113.7 %all-reduce.9.cloned.1.call-start = ((), (), s32[]{:S(2)}) async-start(), calls=%async_computation.1 | async-start | bytes 2097152 | tf_op jit(solution)/shard_map/psum | solution.py:37
  180.0 108.5 %all-gather.17.cloned.1.call-start = ((), (), s32[]{:S(2)}) async-start(), calls=%async_computation.8 | async-start | bytes 2228224 | tf_op jit(solution)/shard_map/all_gather | solution.py:15
  243.9 113.0 %all-reduce.11.cloned.1.call-start = ((), (), s32[]{:S(2)}) async-start(), calls=%async_computation.2 | async-start | bytes 2097152 | tf_op jit(solution)/shard_map/psum | solution.py:37
  294.7 86.9 %all-gather.19.cloned.1.call-start = ((), (), s32[]{:S(2)}) async-start(), calls=%async_computation.9 | async-start | bytes 1179648 | tf_op jit(solution)/shard_map/all_gather | solution.py:23
  358.8 121.4 %all-reduce.13.cloned.1.call-start = ((), (), s32[]{:S(2)}) async-start(), calls=%async_computation.3 | async-start | bytes 4194304 | tf_op jit(solution)/shard_map/psum | solution.py:43
  381.6 98.7 %copy-start.2 = (bf16[512,128]{0,1:T(8,128)(2,1)S(1)}, bf16[512,128]{0,1:T(8,128)(2,1)}, u32[]{:S(2)}) copy-start(bf16[512,128]{0,1:T(8,128)(2,1)} %convolution_convert_fusion.4) | copy-start | bytes 393220
  387.9 117.0 %all-gather.21.cloned.1.call-start = ((), (), s32[]{:S(2)}) async-start(), calls=%async_computation.10 | async-start | bytes 1179648 | tf_op jit(solution)/shard_map/all_gather | solution.py:23
  482.0 121.4 %all-reduce.15.cloned.1.call-start = ((), (), s32[]{:S(2)}) async-start(), calls=%async_computation.4 | async-start | bytes 4194304 | tf_op jit(solution)/shard_map/psum | solution.py:43
  504.9 98.6 %copy-start.1 = (bf16[512,128]{0,1:T(8,128)(2,1)S(1)}, bf16[512,128]{0,1:T(8,128)(2,1)}, u32[]{:S(2)}) copy-start(bf16[512,128]{0,1:T(8,128)(2,1)} %convolution_convert_fusion.5) | copy-start | bytes 393220
  511.2 117.0 %all-gather.23.cloned.1.call-start = ((), (), s32[]{:S(2)}) async-start(), calls=%async_computation.11 | async-start | bytes 1179648 | tf_op jit(solution)/shard_map/all_gather | solution.py:23
  605.3 121.5 %all-reduce.17.cloned.1.call-start = ((), (), s32[]{:S(2)}) async-start(), calls=%async_computation.5 | async-start | bytes 4194304 | tf_op jit(solution)/shard_map/psum | solution.py:43
  628.1 6.3 copy-start
  628.1 99.8 %copy-start.3 = (bf16[512,128]{1,0:T(8,128)(2,1)S(1)}, bf16[512,128]{1,0:T(8,128)(2,1)}, u32[]{:S(2)}) copy-start(bf16[512,128]{1,0:T(8,128)(2,1)} %convolution_convert_fusion.9) | copy-start | bytes 393220
  628.1 99.8 %copy-start.4 = (bf16[512,128]{1,0:T(8,128)(2,1)S(1)}, bf16[512,128]{1,0:T(8,128)(2,1)}, u32[]{:S(2)}) copy-start(bf16[512,128]{1,0:T(8,128)(2,1)} %convolution_convert_fusion.8) | copy-start | bytes 393220
  628.2 99.8 %copy-start.5 = (bf16[512,128]{1,0:T(8,128)(2,1)S(1)}, bf16[512,128]{1,0:T(8,128)(2,1)}, u32[]{:S(2)}) copy-start(bf16[512,128]{1,0:T(8,128)(2,1)} %convolution_convert_fusion.7) | copy-start | bytes 393220
Sparse Core Ops, SparseCore 0:
  10.7 47.4 all-gather.12
  64.6 61.9 all-reduce.6
  129.4 44.3 all-gather.14
  180.1 61.9 all-reduce.8
  244.1 44.3 all-gather.16
  294.8 61.9 all-reduce.10
  358.9 22.6 all-gather.18
  388.0 92.1 all-reduce.12
  482.2 22.6 all-gather.20
  511.3 92.1 all-reduce.14
  605.4 22.6 all-gather.22
  634.6 92.1 all-reduce.16
where the time goes:
time: 737 us; the launch traced here: 736 us
  waiting for transfers between devices  591 us (80%)
  local copies, waits for them, and re-layouts  50 us (7%)
  matrix products  49.3 us (7%)
  other arithmetic  30.3 us (4%)
  between operations  14.3 us (2%)
    psum x3, waiting for transfers between devices, backward_sum(): summed = lax.psum(blocks.astype(jnp.bfloat16), 'row').astype(jnp.float32)  276 us
    psum x3, waiting for transfers between devices, forward_sum(): lax.psum(blocks.astype(jnp.bfloat16), ('depth', 'col')).astype(jnp.float32)  186 us
    all_gather x3, waiting for transfers between devices, lift_upward(): portion = lax.all_gather(share_in, 'row', axis=0, tiled=True)  94.9 us
    all_gather x3, waiting for transfers between devices, carry_downward(): portion = lax.all_gather(share_in, ('depth', 'col'), axis=1, tiled=True)  33.9 us
    mul x6, local copies, waits for them, and re-layouts, body(): slab.reshape(gate.shape[0], block_width, gate.shape[1], block_width)  29.7 us
    dot_general x3, local copies, waits for them, and re-layouts, carry_downward(): lax.dot_general(masked, portion.reshape(span_rows, portion.shape[-1]), ((...  19.2 us
    dot_general x3, matrix products, carry_downward(): lax.dot_general(masked, portion.reshape(span_rows, portion.shape[-1]), ((...  18.8 us
    dot_general x3, matrix products, lift_upward(): jnp.dot(masked, portion.reshape(span_rows, portion.shape[-1]), preferred_...  18.6 us
  transfers between devices with their start and end apart: 12, of which 12 were waited for; matrix products, arithmetic and copies ran while one was open for 11% of the time, Pallas kernels for 0%

commit v1 on v0

--- a/solution.py
+++ b/solution.py
@@ -31,10 +31,16 @@
 
 
 def forward_sum(partial_value, share_rows):
+
+    def flows_carry(my_tile):
+        for pp in ("col", "depth"):
+            my_tile = lax.psum(my_tile, pp)
+        return my_tile
+
     blocks = partial_value.reshape(
         lax.axis_size(("depth", "col")), share_rows, partial_value.shape[-1]
     )
-    summed = lax.psum(blocks.astype(jnp.bfloat16), ("depth", "col")).astype(jnp.float32)
+    summed = flows_carry(blocks.astype(jnp.bfloat16)).astype(jnp.float32)
     return lax.dynamic_index_in_dim(summed, lax.axis_index(("depth", "col")), 0, keepdims=False)
 
 

time: 737 us -> 778 us (1.056)
  waiting for transfers between devices: 591 us -> 632 us
    psum x3 -> x6, waiting for transfers between devices: 186 us -> 221 us  [flows_carry(): my_tile = lax.psum(my_tile, pp)]
  transfers between devices with their start and end apart: 12 -> 15, of which waited for: 12 -> 15; matrix products, arithmetic and copies ran while one was open for 11% -> 10% of each run, Pallas kernels for 0% -> 0%
where the time goes in v1:
time: 778 us; the launch traced here: 777 us
  waiting for transfers between devices  632 us (81%)
  local copies, waits for them, and re-layouts  50 us (6%)
  matrix products  49.3 us (6%)
  other arithmetic  30.3 us (4%)
  between operations  14 us (2%)
    psum x3, waiting for transfers between devices, backward_sum(): summed = lax.psum(blocks.astype(jnp.bfloat16), 'row').astype(jnp.float32)  276 us
    psum x6, waiting for transfers between devices, flows_carry(): my_tile = lax.psum(my_tile, pp)  221 us
    all_gather x3, waiting for transfers between devices, lift_upward(): portion = lax.all_gather(share_in, 'row', axis=0, tiled=True)  99 us
    all_gather x3, waiting for transfers between devices, carry_downward(): portion = lax.all_gather(share_in, ('depth', 'col'), axis=1, tiled=True)  36 us
    mul x6, local copies, waits for them, and re-layouts, body(): slab.reshape(gate.shape[0], block_width, gate.shape[1], block_width)  29.7 us
    dot_general x3, local copies, waits for them, and re-layouts, carry_downward(): lax.dot_general(masked, portion.reshape(span_rows, portion.shape[-1]), ((...  19.2 us
    dot_general x3, matrix products, carry_downward(): lax.dot_general(masked, portion.reshape(span_rows, portion.shape[-1]), ((...  18.8 us
    dot_general x3, matrix products, lift_upward(): jnp.dot(masked, portion.reshape(span_rows, portion.shape[-1]), preferred_...  18.6 us
  transfers between devices with their start and end apart: 15, of which 15 were waited for; matrix products, arithmetic and copies ran while one was open for 10% of the time, Pallas kernels for 0%

profile of v1, /device:TPU:0, one launch (start us, length us, event | category | flops | bytes accessed | tf_op | source)
XLA Modules:
  0.0 776.8 jit_solution(1784368637754186958)
XLA Ops:
  12.3 7.3 mul.63
  22.2 7.3 mul.72
  32.2 7.4 mul.68
  39.5 13.6 %slice_multiply_fusion.2 = (bf16[1,1,1024,1,2048]{4,2,3,1,0:T(8,128)(2,1)}, bf16[1,1,1024,1,2048]{4,2,3,1,0:T(8,128)(2,1)}, bf16[1,1,1024,1,2048]{4,2,3,1,0:T(8,128)(2,1)}) fusion(bf16[1,1,1024,1,2048]{4,2,3,1,0:T(8,128)(2,1)} %mul.63, bf16[3,1,1024,1,2048]{4,2,3,1,0:T(8,128)(2,1)} %param.6, bf16[1,1,1024,1,2048]{4,2,3,1,0:T(8,128)(2,1)} %mul.72, ...), kind=kLoop, calls=%fused_computation.8 | loop fusion | flops 6291456 | bytes 37748736 | tf_op jit(solution)/shard_map/mul | solution.py:63
  64.5 45.4 %all-reduce.10.cloned.1.call-done = bf16[8,128,512]{2,1,0:T(8,128)(2,1)} async-done(((bf16[8,128,512]{2,1,0:T(8,128)(2,1)}), bf16[8,128,512]{2,1,0:T(8,128)(2,1)}) %all-reduce.10.cloned.1.call-update) | async-done | bytes 1048592 | tf_op jit(solution)/shard_map/psum | solution.py:37
  110.0 28.3 %all-reduce.12.cloned.1.call-done = bf16[8,128,512]{2,1,0:T(8,128)(2,1)} async-done(((bf16[8,128,512]{2,1,0:T(8,128)(2,1)}), bf16[8,128,512]{2,1,0:T(8,128)(2,1)}) %all-reduce.12.cloned.1.call-update) | async-done | bytes 1048592 | tf_op jit(solution)/shard_map/psum | solution.py:37
  140.2 47.2 %all-gather.15.cloned.1.call-done = bf16[2048,512]{1,0:T(8,128)(2,1)} async-done(((bf16[128,512]{1,0:T(8,128)(2,1)}), bf16[2048,512]{1,0:T(8,128)(2,1)}) %all-gather.15.cloned.1.call-update) | async-done | bytes 2097168 | tf_op jit(solution)/shard_map/all_gather | solution.py:15
  193.6 45.4 %all-reduce.14.cloned.1.call-done = bf16[8,128,512]{2,1,0:T(8,128)(2,1)} async-done(((bf16[8,128,512]{2,1,0:T(8,128)(2,1)}), bf16[8,128,512]{2,1,0:T(8,128)(2,1)}) %all-reduce.14.cloned.1.call-update) | async-done | bytes 1048592 | tf_op jit(solution)/shard_map/psum | solution.py:37
  239.1 28.2 %all-reduce.16.cloned.1.call-done = bf16[8,128,512]{2,1,0:T(8,128)(2,1)} async-done(((bf16[8,128,512]{2,1,0:T(8,128)(2,1)}), bf16[8,128,512]{2,1,0:T(8,128)(2,1)}) %all-reduce.16.cloned.1.call-update) | async-done | bytes 1048592 | tf_op jit(solution)/shard_map/psum | solution.py:37
  269.1 46.7 %all-gather.17.cloned.1.call-done = bf16[2048,512]{1,0:T(8,128)(2,1)} async-done(((bf16[128,512]{1,0:T(8,128)(2,1)}), bf16[2048,512]{1,0:T(8,128)(2,1)}) %all-gather.17.cloned.1.call-update) | async-done | bytes 2097168 | tf_op jit(solution)/shard_map/all_gather | solution.py:15
  322.1 45.5 %all-reduce.18.cloned.1.call-done = bf16[8,128,512]{2,1,0:T(8,128)(2,1)} async-done(((bf16[8,128,512]{2,1,0:T(8,128)(2,1)}), bf16[8,128,512]{2,1,0:T(8,128)(2,1)}) %all-reduce.18.cloned.1.call-update) | async-done | bytes 1048592 | tf_op jit(solution)/shard_map/psum | solution.py:37
  367.6 28.3 %all-reduce.20.cloned.1.call-done = bf16[8,128,512]{2,1,0:T(8,128)(2,1)} async-done(((bf16[8,128,512]{2,1,0:T(8,128)(2,1)}), bf16[8,128,512]{2,1,0:T(8,128)(2,1)}) %all-reduce.20.cloned.1.call-update) | async-done | bytes 1048592 | tf_op jit(solution)/shard_map/psum | solution.py:37
  398.2 15.0 %fusion.2 = (bf16[2048,1024]{0,1:T(8,128)(2,1)}, bf16[2048,1024]{0,1:T(8,128)(2,1)}, bf16[2048,1024]{0,1:T(8,128)(2,1)}) fusion(bf16[128,8,16,128]{3,2,1,0:T(8,128)(2,1)} %bitcast.180, bf16[3,1,1024,1,2048]{4,2,3,1,0:T(8,128)(2,1)} %param.6, bf16[128,8,16,128]{3,2,1,0:T(8,128)(2,1)} %bitcast.182, bf16[128,8,16,128]{3,2,1,0:T(8,128)(2,1)} %bitcast.181), kind=kLoop, calls=%fused_computation.5 | loop fusion | flops 6291456 | bytes 37748736 | tf_op jit(solution)/shard_map/dot_general | solution.py:25
  413.2 6.4 copy.26
  422.7 6.3 convolution_convert_fusion.2
  429.1 92.3 %all-reduce.22.cloned.1.call-done = bf16[16,128,512]{2,1,0:T(8,128)(2,1)} async-done(((bf16[16,128,512]{2,1,0:T(8,128)(2,1)}), bf16[16,128,512]{2,1,0:T(8,128)(2,1)}) %all-reduce.22.cloned.1.call-update) | async-done | bytes 2097168 | tf_op jit(solution)/shard_map/psum | solution.py:49
  523.2 6.4 copy.25
  529.6 16.4 %all-gather.21.cloned.1.call-done = bf16[1024,512]{0,1:T(8,128)(2,1)} async-done(((bf16[128,512]{0,1:T(8,128)(2,1)}), bf16[1024,512]{0,1:T(8,128)(2,1)}) %all-gather.21.cloned.1.call-update) | async-done | bytes 1048592 | tf_op jit(solution)/shard_map/all_gather | solution.py:23
  546.0 6.3 convolution_convert_fusion.1
  552.4 92.3 %all-reduce.24.cloned.1.call-done = bf16[16,128,512]{2,1,0:T(8,128)(2,1)} async-done(((bf16[16,128,512]{2,1,0:T(8,128)(2,1)}), bf16[16,128,512]{2,1,0:T(8,128)(2,1)}) %all-reduce.24.cloned.1.call-update) | async-done | bytes 2097168 | tf_op jit(solution)/shard_map/psum | solution.py:49
  646.5 6.4 copy.24
  652.9 16.4 %all-gather.23.cloned.1.call-done = bf16[1024,512]{0,1:T(8,128)(2,1)} async-done(((bf16[128,512]{0,1:T(8,128)(2,1)}), bf16[1024,512]{0,1:T(8,128)(2,1)}) %all-gather.23.cloned.1.call-update) | async-done | bytes 1048592 | tf_op jit(solution)/shard_map/all_gather | solution.py:23
  669.3 6.3 convolution_convert_fusion
  676.5 91.5 %all-reduce.26.cloned.1.call-done = bf16[16,128,512]{2,1,0:T(8,128)(2,1)} async-done(((bf16[16,128,512]{2,1,0:T(8,128)(2,1)}), bf16[16,128,512]{2,1,0:T(8,128)(2,1)}) %all-reduce.26.cloned.1.call-update) | async-done | bytes 2097168 | tf_op jit(solution)/shard_map/psum | solution.py:49
  (67 shorter events, 50.3 us)
Async XLA Ops:
  7.2 51.1 %all-gather.13.cloned.1.call-start = ((), (), s32[]{:S(2)}) async-start(), calls=%async_computation.9 | async-start | bytes 2228224 | tf_op jit(solution)/shard_map/all_gather | solution.py:15
  9.0 101.0 %all-reduce.10.cloned.1.call-start = ((), (), s32[]{:S(2)}) async-start(), calls=%async_computation | async-start | bytes 2097152 | tf_op jit(solution)/shard_map/psum | solution.py:37
  58.2 80.1 %copy-start.6 = (bf16[4,1,1,128,512]{4,3,2,1,0:T(8,128)(2,1)S(1)}, bf16[4,1,1,128,512]{4,3,2,1,0:T(8,128)(2,1)}, u32[]{:S(2)}) copy-start(bf16[4,1,1,128,512]{4,3,2,1,0:T(8,128)(2,1)} %param.4) | copy-start | bytes 1572868
  58.2 80.1 %copy-start.7 = (bf16[4,1,1,1,128,128]{5,4,3,2,1,0:T(8,128)(2,1)S(1)}, bf16[4,1,1,1,128,128]{5,4,3,2,1,0:T(8,128)(2,1)}, u32[]{:S(2)}) copy-start(bf16[4,1,1,1,128,128]{5,4,3,2,1,0:T(8,128)(2,1)} %param.5) | copy-start | bytes 393220
  64.5 73.9 %all-reduce.12.cloned.1.call-start = ((), (), s32[]{:S(2)}) async-start(), calls=%async_computation.1 | async-start | bytes 2097152 | tf_op jit(solution)/shard_map/psum | solution.py:37
  110.0 77.4 %all-gather.15.cloned.1.call-start = ((), (), s32[]{:S(2)}) async-start(), calls=%async_computation.10 | async-start | bytes 2228224 | tf_op jit(solution)/shard_map/all_gather | solution.py:15
  140.1 98.9 %all-reduce.14.cloned.1.call-start = ((), (), s32[]{:S(2)}) async-start(), calls=%async_computation.2 | async-start | bytes 2097152 | tf_op jit(solution)/shard_map/psum | solution.py:37
  193.6 73.7 %all-reduce.16.cloned.1.call-start = ((), (), s32[]{:S(2)}) async-start(), calls=%async_computation.3 | async-start | bytes 2097152 | tf_op jit(solution)/shard_map/psum | solution.py:37
  239.0 76.8 %all-gather.17.cloned.1.call-start = ((), (), s32[]{:S(2)}) async-start(), calls=%async_computation.11 | async-start | bytes 2228224 | tf_op jit(solution)/shard_map/all_gather | solution.py:15
  269.0 98.5 %all-reduce.18.cloned.1.call-start = ((), (), s32[]{:S(2)}) async-start(), calls=%async_computation.4 | async-start | bytes 2097152 | tf_op jit(solution)/shard_map/psum | solution.py:37
  322.0 73.9 %all-reduce.20.cloned.1.call-start = ((), (), s32[]{:S(2)}) async-start(), calls=%async_computation.5 | async-start | bytes 2097152 | tf_op jit(solution)/shard_map/psum | solution.py:37
  367.6 55.2 %all-gather.19.cloned.1.call-start = ((), (), s32[]{:S(2)}) async-start(), calls=%async_computation.12 | async-start | bytes 1179648 | tf_op jit(solution)/shard_map/all_gather | solution.py:23
  397.9 123.5 %all-reduce.22.cloned.1.call-start = ((), (), s32[]{:S(2)}) async-start(), calls=%async_computation.6 | async-start | bytes 4194304 | tf_op jit(solution)/shard_map/psum | solution.py:49
  422.7 98.7 %copy-start.2 = (bf16[512,128]{0,1:T(8,128)(2,1)S(1)}, bf16[512,128]{0,1:T(8,128)(2,1)}, u32[]{:S(2)}) copy-start(bf16[512,128]{0,1:T(8,128)(2,1)} %convolution_convert_fusion.4) | copy-start | bytes 393220
  429.0 117.0 %all-gather.21.cloned.1.call-start = ((), (), s32[]{:S(2)}) async-start(), calls=%async_computation.13 | async-start | bytes 1179648 | tf_op jit(solution)/shard_map/all_gather | solution.py:23
  523.2 121.5 %all-reduce.24.cloned.1.call-start = ((), (), s32[]{:S(2)}) async-start(), calls=%async_computation.7 | async-start | bytes 4194304 | tf_op jit(solution)/shard_map/psum | solution.py:49
  546.0 98.6 %copy-start.1 = (bf16[512,128]{0,1:T(8,128)(2,1)S(1)}, bf16[512,128]{0,1:T(8,128)(2,1)}, u32[]{:S(2)}) copy-start(bf16[512,128]{0,1:T(8,128)(2,1)} %convolution_convert_fusion.5) | copy-start | bytes 393220
  552.3 117.0 %all-gather.23.cloned.1.call-start = ((), (), s32[]{:S(2)}) async-start(), calls=%async_computation.14 | async-start | bytes 1179648 | tf_op jit(solution)/shard_map/all_gather | solution.py:23
  646.4 121.5 %all-reduce.26.cloned.1.call-start = ((), (), s32[]{:S(2)}) async-start(), calls=%async_computation.8 | async-start | bytes 4194304 | tf_op jit(solution)/shard_map/psum | solution.py:49
  669.3 6.3 copy-start
  669.3 99.8 %copy-start.3 = (bf16[512,128]{1,0:T(8,128)(2,1)S(1)}, bf16[512,128]{1,0:T(8,128)(2,1)}, u32[]{:S(2)}) copy-start(bf16[512,128]{1,0:T(8,128)(2,1)} %convolution_convert_fusion.9) | copy-start | bytes 393220
  669.3 99.8 %copy-start.4 = (bf16[512,128]{1,0:T(8,128)(2,1)S(1)}, bf16[512,128]{1,0:T(8,128)(2,1)}, u32[]{:S(2)}) copy-start(bf16[512,128]{1,0:T(8,128)(2,1)} %convolution_convert_fusion.8) | copy-start | bytes 393220
  669.3 99.8 %copy-start.5 = (bf16[512,128]{1,0:T(8,128)(2,1)S(1)}, bf16[512,128]{1,0:T(8,128)(2,1)}, u32[]{:S(2)}) copy-start(bf16[512,128]{1,0:T(8,128)(2,1)} %convolution_convert_fusion.7) | copy-start | bytes 393220
Sparse Core Ops, SparseCore 0:
  10.7 47.4 all-gather.12
  64.6 45.3 all-reduce.9
  112.4 25.8 all-reduce.11
  140.9 46.3 all-gather.14
  193.7 45.2 all-reduce.13
  241.3 25.8 all-reduce.15
  269.4 46.3 all-gather.16
  322.2 45.3 all-reduce.17
  370.0 25.8 all-reduce.19
  398.1 24.6 all-gather.18
  429.2 92.1 all-reduce.21
  523.3 22.6 all-gather.20
  552.5 92.1 all-reduce.23
  646.6 22.6 all-gather.22
  675.7 92.1 all-reduce.25
